TPU v7x, 32 devices: a whole 2x2x4 slice. The times are simulated.
32 devices in a mesh: section: 2 (over x), expert: 4 (over z), tensor: 4 (over y, core).
Axes of the slice: x: 2, y: 2, z: 4, core: 2. Of those that a mesh axis runs over, the one named last changes fastest.
Arguments:
- layer_inputs: bfloat16 [2, 2, 320, 3072], P('section', None, 'expert', 'tensor'), may hold values from -6 to 6
- grad_out: bfloat16 [2, 320, 3072], P(None, 'expert', 'tensor'), may hold values from -6 to 6
- norm_gain: bfloat16 [2, 3072], P('section', 'tensor'), may hold values from 0.25 to 1.75
- router_w: bfloat16 [2, 3072, 4], P('section', 'tensor'), may hold values from -0.21875 to 0.21875
- w_gate: bfloat16 [2, 3072, 32768], P('section', None, ('expert', 'tensor')), may hold values from -0.109375 to 0.109375
- w_up: bfloat16 [2, 3072, 32768], P('section', None, ('expert', 'tensor')), may hold values from -0.109375 to 0.109375
- w_down: bfloat16 [2, 32768, 3072], P('section', ('expert', 'tensor')), may hold values from -0.0625 to 0.0625
- saved_gate: bfloat16 [2, 2, 4, 64, 32768], P('section', None, None, None, ('expert', 'tensor')), may hold values from -6 to 6
- saved_up: bfloat16 [2, 2, 4, 64, 32768], P('section', None, None, None, ('expert', 'tensor')), may hold values from -6 to 6
- routes: int32 [2, 2, 320, 2], P('section', None, 'expert'), may hold values from 0 to 3, all different within a row; in each aligned block of 80 rows (0 to 79, 80 to 159, ..., all dimensions but the last counted through in order) at most 64 rows name the same one
Outputs:
- layer_grads: bfloat16 [2, 2, 320, 3072], P('section', None, 'expert', 'tensor')
Inputs may be any that keep to these rules, and one draw needn't show every extreme that they name: `routes`: each token names two different experts; within the 80 tokens of one device's aligned block of a layer and micro-batch, no expert is named by more than 64 tokens, and in some blocks one expert is named by exactly 64.
All inputs are finite; a program needn't handle non-finite values.
Results may differ from a plain program's by a relative error of at most 0.011.
Values may be sent and summed in bfloat16 or wider, within the bound.
A program may use at most 128 MiB of HBM per device.

v0:
```python
import jax
import jax.numpy as jnp
from jax import lax
from jax.sharding import PartitionSpec as P

norm_eps = 1e-05
highest = lax.Precision.HIGHEST


def from_behind(block, axis, distance):
    devices = range(lax.axis_size(axis))
    route = [(i - distance, i) for i in devices if i - distance in devices]
    return lax.ppermute(block, axis, route)


def on_device(
    layer_inputs, grad_out, norm_gain, router_w, w_gate, w_up, w_down, saved_gate, saved_up, routes
):
    sections = lax.axis_size("section")
    position = lax.axis_index("section")
    holders = lax.axis_size("expert")
    micros = grad_out.shape[0]
    tokens_here = grad_out.shape[1]
    quarter = grad_out.shape[2]
    gain_full = norm_gain[0].astype(jnp.float32)
    router = router_w[0]
    gate_mat = w_gate[0]
    up_mat = w_up[0]
    down_mat = w_down[0]
    width_all = gate_mat.shape[0]
    experts = router.shape[1]
    group = holders // experts
    capacity = saved_gate.shape[3]
    slot_count = experts * capacity
    slot_ids = jnp.arange(slot_count, dtype=jnp.int32)
    expert_ids = jnp.arange(experts, dtype=jnp.int32)

    def add_columns(piece):
        return jnp.einsum("scw,fw->scf", piece, down_mat, preferred_element_type=jnp.float32)

    def layer_back(inputs, upstream, chosen, gate_saved, up_saved):
        values = inputs.astype(jnp.float32)
        squares = lax.psum(jnp.sum(values * values, axis=-1), "tensor")
        scale = lax.rsqrt(squares / width_all + norm_eps)[:, None]
        normed = (values * scale * gain_full).astype(jnp.bfloat16)
        partial_logits = jnp.dot(normed, router, preferred_element_type=jnp.float32)
        logits = lax.psum(partial_logits, "tensor")
        onehot = (chosen[:, :, None] == expert_ids[None, None, :]).astype(jnp.float32)
        picked = jnp.sum(onehot * logits[:, None, :], axis=-1)
        first = jax.nn.sigmoid(picked[:, 0] - picked[:, 1])
        second = jax.nn.sigmoid(picked[:, 1] - picked[:, 0])
        flat_hot = onehot.reshape(tokens_here * 2, experts)
        earlier = jnp.cumsum(flat_hot, axis=0) - flat_hot
        within = jnp.sum(earlier * flat_hot, axis=-1).astype(jnp.int32)
        target = chosen.reshape(tokens_here * 2) * capacity + within
        placing = (
            (slot_ids[:, None] == target[None, :])
            .astype(jnp.float32)
            .reshape(slot_count, tokens_here, 2)
        )
        select = jnp.sum(placing, axis=-1).astype(jnp.bfloat16)
        upstream_send = jnp.dot(select, upstream, preferred_element_type=jnp.float32).astype(
            jnp.bfloat16
        )
        copies = jnp.broadcast_to(
            upstream_send.reshape(experts, 1, capacity, quarter),
            (experts, group, capacity, quarter),
        ).reshape(holders, capacity, quarter)
        arrived = lax.all_to_all(copies, "expert", split_axis=0, concat_axis=0, tiled=True)
        back_act = add_columns(lax.all_gather(arrived, "tensor", axis=2, tiled=True))
        gate_act = gate_saved.astype(jnp.float32)
        up_act = up_saved.astype(jnp.float32)
        sigma = jax.nn.sigmoid(gate_act)
        swish = gate_act * sigma
        weight_part = jnp.sum(swish * up_act * back_act, axis=-1)
        slope = sigma * (1.0 + gate_act * (1.0 - sigma))
        gate_grad = (back_act * up_act * slope).astype(jnp.bfloat16)
        up_grad = (back_act * swish).astype(jnp.bfloat16)
        unit = jnp.einsum("scf,df->scd", gate_grad, gate_mat, preferred_element_type=jnp.float32)
        unit = unit + jnp.einsum("scf,df->scd", up_grad, up_mat, preferred_element_type=jnp.float32)
        weighted = placing[:, :, 0] * first[None, :] + placing[:, :, 1] * second[None, :]
        unit_share = lax.psum_scatter(unit, "tensor", scatter_dimension=2, tiled=True)
        back_units, back_weights = (
            lax.all_to_all(unit_share, "expert", split_axis=0, concat_axis=0, tiled=True),
            lax.all_to_all(weight_part, "expert", split_axis=0, concat_axis=0, tiled=True),
        )
        slot_units = jnp.sum(back_units.reshape(experts, group, capacity, quarter), axis=1).reshape(
            slot_count, quarter
        )
        slot_weight = jnp.sum(back_weights.reshape(experts, group, capacity), axis=1).reshape(
            slot_count
        )
        hidden_grad = lax.dot_general(
            weighted, slot_units, (((0,), (0,)), ((), ())), precision=highest
        )
        prob_part = jnp.einsum("stk,s->tk", placing, slot_weight, precision=highest)
        prob_grad = lax.psum(prob_part, "tensor")
        logit_step = first * second * (prob_grad[:, 0] - prob_grad[:, 1])
        logit_grad = (onehot[:, 0, :] - onehot[:, 1, :]) * logit_step[:, None]
        hidden_grad = hidden_grad + jnp.einsum(
            "te,de->td", logit_grad, router.astype(jnp.float32), precision=highest
        )
        gained = hidden_grad * gain_full
        moment = lax.psum(jnp.sum(values * gained, axis=-1), "tensor")[:, None] / width_all
        result = (
            upstream.astype(jnp.float32) + scale * gained - values * scale * scale * scale * moment
        )
        return result.astype(jnp.bfloat16)

    def advance(tick, carry):
        incoming, grads = carry
        micro_id = tick - (sections - 1 - position)
        valid = jnp.logical_and(micro_id >= 0, micro_id < micros)
        safe_id = jnp.clip(micro_id, 0, micros - 1)
        inputs = lax.dynamic_index_in_dim(layer_inputs[0], safe_id, 0, keepdims=False)
        top_grad = lax.dynamic_index_in_dim(grad_out, safe_id, 0, keepdims=False)
        chosen = lax.dynamic_index_in_dim(routes[0], safe_id, 0, keepdims=False)
        gate_saved = lax.dynamic_index_in_dim(saved_gate[0], safe_id, 0, keepdims=False)
        up_saved = lax.dynamic_index_in_dim(saved_up[0], safe_id, 0, keepdims=False)
        upstream = jnp.where(position == sections - 1, top_grad, incoming)
        computed = layer_back(inputs, upstream, chosen, gate_saved, up_saved)
        result = jnp.where(valid, computed, jnp.zeros_like(computed))
        updated = lax.dynamic_update_index_in_dim(grads, result, safe_id, 0)
        grads = jnp.where(valid, updated, grads)
        incoming = from_behind(result, "section", -1)
        return (incoming, grads)

    start = (
        jnp.zeros((tokens_here, quarter), jnp.bfloat16),
        jnp.zeros((micros, tokens_here, quarter), jnp.bfloat16),
    )
    final_in, grads = lax.fori_loop(0, micros + sections - 1, advance, start)
    return grads[None]


def solution(mesh):
    placed = (
        P("section", None, "expert", "tensor"),
        P(None, "expert", "tensor"),
        P("section", "tensor"),
        P("section", "tensor", None),
        P("section", None, ("expert", "tensor")),
        P("section", None, ("expert", "tensor")),
        P("section", ("expert", "tensor"), None),
        P("section", None, None, None, ("expert", "tensor")),
        P("section", None, None, None, ("expert", "tensor")),
        P("section", None, "expert", None),
    )
    return jax.shard_map(
        on_device,
        mesh=mesh,
        in_specs=placed,
        out_specs=P("section", None, "expert", "tensor"),
        check_vma=False,
    )
```

profile of v0, /device:TPU:0, one launch (start us, length us, event | category | flops | bytes accessed | tf_op | source)
XLA Modules:
  0.0 453.6 jit_solution(15014488951981677367)
XLA Ops:
  7.3 438.8 %while.19 = (s32[]{:T(128)}, bf16[80,768]{1,0:T(8,128)(2,1)S(1)}, bf16[2,80,768]{2,1,0:T(8,128)(2,1)S(1)}, s32[]{:T(128)}, pred[]{:T(512)}, /*index=5*/bf16[2,80...) while((s32[]{:T(128)}, bf16[80,768]{1,0:T(8,128)(2,1)S(1)}, ...), condition=%wide.region_14.15_spmd.clone.clone, body=%wide.region_0.14_spmd.clone.clone.sunk | while | flops 9905498112 | bytes 112821912 | solution.py:132
  8.5 1.2 reduce-window.24
  12.3 17.9 %all_to_all.47 = bf16[4,64,768]{2,1,0:T(8,128)(2,1)} all-to-all(bf16[4,64,768]{2,1,0:T(8,128)(2,1)S(1)} %bitcast.166), channel_id=1, replica_groups=mesh['section'=2,'expert'=4,'tensor'=4] {'expert'}, dimensions={0} | all-to-all | bytes 786432 | tf_op jit(solution)/shard_map/while/body/eval_jaxpr/all_to_all | solution.py:69
  30.3 18.8 %all-gather.2.cloned.1.call-done = bf16[4,64,3072]{2,1,0:T(8,128)(2,1)} async-done(((bf16[4,64,768]{2,1,0:T(8,128)(2,1)}), bf16[4,64,3072]{2,1,0:T(8,128)(2,1)}) %all-gather.2.cloned.1.call-update) | async-done | bytes 1572880 | tf_op jit(solution)/shard_map/while/body/eval_jaxpr/all_gather | solution.py:70
  49.2 9.9 %fusion.123 = (f32[4,64]{1,0:T(4,128)}, f32[4,64,2048]{2,1,0:T(8,128)S(1)}) fusion(bf16[1,2,4,64,2048]{4,3,2,1,0:T(8,128)(2,1)S(1)} %copy-done.5, s32[]{:T(128)S(6)} %min.13, bf16[1,2,4,64,2048]{4,3,2,1,0:T(8,128)(2,1)} %get-tuple-element.699, bf16[4,64,3072]{2,1,0:T(8,128)(2,1)} %all-gather.2.cloned.1.call-done, ...), kind=kOutput, calls=%fused_computation.17.clone.1 | convolution fusion | flops 3225943808 | bytes 18351108 | tf_op jit(solution)/shard_map/while/body/eval_jaxpr/scw,fw->scf/dot_general | solution.py:39
  59.1 10.7 %fusion.129 = f32[4,64,3072]{2,1,0:T(8,128)} fusion(bf16[3072,2048]{1,0:T(8,128)(2,1)} %get-tuple-element.701, f32[4,64,2048]{2,1,0:T(8,128)S(1)} %get-tuple-element.640, bf16[1,2,4,64,2048]{4,3,2,1,0:T(8,128)(2,1)S(1)} %copy-done.6, s32[]{:T(128)S(6)} %min.13), kind=kOutput, calls=%fused_computation.2.clone.1 | convolution fusion | flops 3224895488 | bytes 18874372 | tf_op jit(solution)/shard_map/while/body/eval_jaxpr/scf,df->scd/dot_general | solution.py:80
  69.8 11.6 %fusion.130 = f32[4,64,3072]{2,1,0:T(8,128)} fusion(f32[4,64,3072]{2,1,0:T(8,128)} %fusion.129, bf16[3072,2048]{1,0:T(8,128)(2,1)} %get-tuple-element.700, f32[4,64,2048]{2,1,0:T(8,128)} %copy-done.7, bf16[1,2,4,64,2048]{4,3,2,1,0:T(8,128)(2,1)S(1)} %copy-done.6, s32[]{:T(128)S(6)} %min.13, bf16[1,2,4,64,2048]{4,3,2,1,0:T(8,128)(2,1)S(1)} %copy-done.5), kind=kOutput, calls=%fused_computation.8.clone.1 | convolution fusion | flops 3228303360 | bytes 23068676 | tf_op jit(solution)/shard_map/while/body/eval_jaxpr/scf,df->scd/dot_general | solution.py:79
  82.5 5.9 %psum.62 = f32[80]{0:T(128)S(1)} all-reduce(f32[80]{0:T(128)S(1)} %fusion.125), channel_id=1, replica_groups=mesh['section'=2,'expert'=4,'tensor'=4] {'tensor'}, use_global_device_ids=true, to_apply=%region_2.2 | all-reduce | flops 80 | bytes 640 | tf_op jit(solution)/shard_map/while/body/eval_jaxpr/psum | solution.py:43
  88.6 4.8 %all-to-all-start.1 = ((f32[4,1,64]{2,1,0:T(1,128)}), f32[4,1,64]{2,1,0:T(1,128)S(1)}, u32[]{:S(2)}, u32[]{:S(2)}) async-start(f32[4,1,64]{2,1,0:T(1,128)} %bitcast.160), calls=%async_computation.1 | async-start | bytes 4096 | tf_op jit(solution)/shard_map/while/body/eval_jaxpr/all_to_all | solution.py:85
  93.3 5.5 %all-to-all-done.1 = f32[4,1,64]{2,1,0:T(1,128)S(1)} async-done(((f32[4,1,64]{2,1,0:T(1,128)}), f32[4,1,64]{2,1,0:T(1,128)S(1)}, u32[]{:S(2)}, u32[]{:S(2)}) %all-to-all-start.1) | async-done | bytes 1056 | tf_op jit(solution)/shard_map/while/body/eval_jaxpr/all_to_all | solution.py:85
  98.8 20.5 %reduce-scatter.2.cloned.1.call-done = f32[4,64,768]{2,1,0:T(8,128)} async-done(((f32[4,64,3072]{2,1,0:T(8,128)}), f32[4,64,768]{2,1,0:T(8,128)}) %reduce-scatter.2.cloned.1.call-update) | async-done | bytes 786448 | tf_op jit(solution)/shard_map/while/body/eval_jaxpr/reduce_scatter | solution.py:82
  119.3 4.6 %all-to-all-start.2 = ((f32[4,64,768]{2,1,0:T(8,128)}), f32[4,64,768]{2,1,0:T(8,128)S(1)}, u32[]{:S(2)}, u32[]{:S(2)}) async-start(f32[4,64,768]{2,1,0:T(8,128)} %reduce-scatter.2.cloned.1.call-done), calls=%async_computation.3 | async-start | bytes 1572864 | tf_op jit(solution)/shard_map/while/body/eval_jaxpr/all_to_all | solution.py:84
  125.5 6.1 %all-reduce.3 = (f32[80,2]{0,1:T(2,128)S(1)}, f32[80,4]{0,1:T(4,128)S(1)}) all-reduce(f32[80,2]{0,1:T(2,128)S(1)} %bitcast.172, f32[80,4]{0,1:T(4,128)S(1)} %fusion.126), channel_id=1, replica_groups=mesh['section'=2,'expert'=4,'tensor'=4] {'tensor'}, use_global_device_ids=true, to_apply=%region_11.11 | all-reduce | flops 480 | bytes 3840 | tf_op jit(solution)/shard_map/while/body/eval_jaxpr/psum | solution.py:97
  131.9 12.0 %all-to-all-done.2 = f32[4,64,768]{2,1,0:T(8,128)S(1)} async-done(((f32[4,64,768]{2,1,0:T(8,128)}), f32[4,64,768]{2,1,0:T(8,128)S(1)}, u32[]{:S(2)}, u32[]{:S(2)}) %all-to-all-start.2) | async-done | bytes 786464 | tf_op jit(solution)/shard_map/while/body/eval_jaxpr/all_to_all | solution.py:84
  144.6 5.9 %psum.63 = f32[80]{0:T(128)S(1)} all-reduce(f32[80]{0:T(128)S(1)} %get-tuple-element.643), channel_id=1, replica_groups=mesh['section'=2,'expert'=4,'tensor'=4] {'tensor'}, use_global_device_ids=true, to_apply=%region_13.13 | all-reduce | flops 80 | bytes 640 | tf_op jit(solution)/shard_map/while/body/eval_jaxpr/psum | solution.py:104
  150.7 1.3 collective-permute-start
  152.0 5.5 %collective-permute-done = bf16[80,768]{1,0:T(8,128)(2,1)S(1)} collective-permute-done((bf16[80,768]{1,0:T(8,128)(2,1)S(1)}, bf16[80,768]{1,0:T(8,128)(2,1)S(1)}, u32[]{:S(2)}, u32[]{:S(2)}) %collective-permute-start) | collective-permute-done | bytes 122912 | tf_op jit(solution)/shard_map/while/body/eval_jaxpr/ppermute | solution.py:13
  158.6 1.2 reduce-window.24
  162.5 13.6 %all_to_all.47 = bf16[4,64,768]{2,1,0:T(8,128)(2,1)} all-to-all(bf16[4,64,768]{2,1,0:T(8,128)(2,1)S(1)} %bitcast.166), channel_id=1, replica_groups=mesh['section'=2,'expert'=4,'tensor'=4] {'expert'}, dimensions={0} | all-to-all | bytes 786432 | tf_op jit(solution)/shard_map/while/body/eval_jaxpr/all_to_all | solution.py:69
  176.2 17.3 %all-gather.2.cloned.1.call-done = bf16[4,64,3072]{2,1,0:T(8,128)(2,1)} async-done(((bf16[4,64,768]{2,1,0:T(8,128)(2,1)}), bf16[4,64,3072]{2,1,0:T(8,128)(2,1)}) %all-gather.2.cloned.1.call-update) | async-done | bytes 1572880 | tf_op jit(solution)/shard_map/while/body/eval_jaxpr/all_gather | solution.py:70
  193.5 9.9 %fusion.123 = (f32[4,64]{1,0:T(4,128)}, f32[4,64,2048]{2,1,0:T(8,128)S(1)}) fusion(bf16[1,2,4,64,2048]{4,3,2,1,0:T(8,128)(2,1)S(1)} %copy-done.5, s32[]{:T(128)S(6)} %min.13, bf16[1,2,4,64,2048]{4,3,2,1,0:T(8,128)(2,1)} %get-tuple-element.699, bf16[4,64,3072]{2,1,0:T(8,128)(2,1)} %all-gather.2.cloned.1.call-done, ...), kind=kOutput, calls=%fused_computation.17.clone.1 | convolution fusion | flops 3225943808 | bytes 18351108 | tf_op jit(solution)/shard_map/while/body/eval_jaxpr/scw,fw->scf/dot_general | solution.py:39
  203.3 10.7 %fusion.129 = f32[4,64,3072]{2,1,0:T(8,128)} fusion(bf16[3072,2048]{1,0:T(8,128)(2,1)} %get-tuple-element.701, f32[4,64,2048]{2,1,0:T(8,128)S(1)} %get-tuple-element.640, bf16[1,2,4,64,2048]{4,3,2,1,0:T(8,128)(2,1)S(1)} %copy-done.6, s32[]{:T(128)S(6)} %min.13), kind=kOutput, calls=%fused_computation.2.clone.1 | convolution fusion | flops 3224895488 | bytes 18874372 | tf_op jit(solution)/shard_map/while/body/eval_jaxpr/scf,df->scd/dot_general | solution.py:80
  214.0 11.6 %fusion.130 = f32[4,64,3072]{2,1,0:T(8,128)} fusion(f32[4,64,3072]{2,1,0:T(8,128)} %fusion.129, bf16[3072,2048]{1,0:T(8,128)(2,1)} %get-tuple-element.700, f32[4,64,2048]{2,1,0:T(8,128)} %copy-done.7, bf16[1,2,4,64,2048]{4,3,2,1,0:T(8,128)(2,1)S(1)} %copy-done.6, s32[]{:T(128)S(6)} %min.13, bf16[1,2,4,64,2048]{4,3,2,1,0:T(8,128)(2,1)S(1)} %copy-done.5), kind=kOutput, calls=%fused_computation.8.clone.1 | convolution fusion | flops 3228303360 | bytes 23068676 | tf_op jit(solution)/shard_map/while/body/eval_jaxpr/scf,df->scd/dot_general | solution.py:79
  226.8 5.9 %psum.62 = f32[80]{0:T(128)S(1)} all-reduce(f32[80]{0:T(128)S(1)} %fusion.125), channel_id=1, replica_groups=mesh['section'=2,'expert'=4,'tensor'=4] {'tensor'}, use_global_device_ids=true, to_apply=%region_2.2 | all-reduce | flops 80 | bytes 640 | tf_op jit(solution)/shard_map/while/body/eval_jaxpr/psum | solution.py:43
  232.8 4.8 %all-to-all-start.1 = ((f32[4,1,64]{2,1,0:T(1,128)}), f32[4,1,64]{2,1,0:T(1,128)S(1)}, u32[]{:S(2)}, u32[]{:S(2)}) async-start(f32[4,1,64]{2,1,0:T(1,128)} %bitcast.160), calls=%async_computation.1 | async-start | bytes 4096 | tf_op jit(solution)/shard_map/while/body/eval_jaxpr/all_to_all | solution.py:85
  237.6 5.5 %all-to-all-done.1 = f32[4,1,64]{2,1,0:T(1,128)S(1)} async-done(((f32[4,1,64]{2,1,0:T(1,128)}), f32[4,1,64]{2,1,0:T(1,128)S(1)}, u32[]{:S(2)}, u32[]{:S(2)}) %all-to-all-start.1) | async-done | bytes 1056 | tf_op jit(solution)/shard_map/while/body/eval_jaxpr/all_to_all | solution.py:85
  243.1 20.5 %reduce-scatter.2.cloned.1.call-done = f32[4,64,768]{2,1,0:T(8,128)} async-done(((f32[4,64,3072]{2,1,0:T(8,128)}), f32[4,64,768]{2,1,0:T(8,128)}) %reduce-scatter.2.cloned.1.call-update) | async-done | bytes 786448 | tf_op jit(solution)/shard_map/while/body/eval_jaxpr/reduce_scatter | solution.py:82
  263.6 4.6 %all-to-all-start.2 = ((f32[4,64,768]{2,1,0:T(8,128)}), f32[4,64,768]{2,1,0:T(8,128)S(1)}, u32[]{:S(2)}, u32[]{:S(2)}) async-start(f32[4,64,768]{2,1,0:T(8,128)} %reduce-scatter.2.cloned.1.call-done), calls=%async_computation.3 | async-start | bytes 1572864 | tf_op jit(solution)/shard_map/while/body/eval_jaxpr/all_to_all | solution.py:84
  269.8 6.1 %all-reduce.3 = (f32[80,2]{0,1:T(2,128)S(1)}, f32[80,4]{0,1:T(4,128)S(1)}) all-reduce(f32[80,2]{0,1:T(2,128)S(1)} %bitcast.172, f32[80,4]{0,1:T(4,128)S(1)} %fusion.126), channel_id=1, replica_groups=mesh['section'=2,'expert'=4,'tensor'=4] {'tensor'}, use_global_device_ids=true, to_apply=%region_11.11 | all-reduce | flops 480 | bytes 3840 | tf_op jit(solution)/shard_map/while/body/eval_jaxpr/psum | solution.py:97
  276.2 11.9 %all-to-all-done.2 = f32[4,64,768]{2,1,0:T(8,128)S(1)} async-done(((f32[4,64,768]{2,1,0:T(8,128)}), f32[4,64,768]{2,1,0:T(8,128)S(1)}, u32[]{:S(2)}, u32[]{:S(2)}) %all-to-all-start.2) | async-done | bytes 786464 | tf_op jit(solution)/shard_map/while/body/eval_jaxpr/all_to_all | solution.py:84
  288.9 5.9 %psum.63 = f32[80]{0:T(128)S(1)} all-reduce(f32[80]{0:T(128)S(1)} %get-tuple-element.643), channel_id=1, replica_groups=mesh['section'=2,'expert'=4,'tensor'=4] {'tensor'}, use_global_device_ids=true, to_apply=%region_13.13 | all-reduce | flops 80 | bytes 640 | tf_op jit(solution)/shard_map/while/body/eval_jaxpr/psum | solution.py:104
  295.0 1.3 collective-permute-start
  296.3 5.5 %collective-permute-done = bf16[80,768]{1,0:T(8,128)(2,1)S(1)} collective-permute-done((bf16[80,768]{1,0:T(8,128)(2,1)S(1)}, bf16[80,768]{1,0:T(8,128)(2,1)S(1)}, u32[]{:S(2)}, u32[]{:S(2)}) %collective-permute-start) | collective-permute-done | bytes 122912 | tf_op jit(solution)/shard_map/while/body/eval_jaxpr/ppermute | solution.py:13
  306.8 13.6 %all_to_all.47 = bf16[4,64,768]{2,1,0:T(8,128)(2,1)} all-to-all(bf16[4,64,768]{2,1,0:T(8,128)(2,1)S(1)} %bitcast.166), channel_id=1, replica_groups=mesh['section'=2,'expert'=4,'tensor'=4] {'expert'}, dimensions={0} | all-to-all | bytes 786432 | tf_op jit(solution)/shard_map/while/body/eval_jaxpr/all_to_all | solution.py:69
  320.5 17.3 %all-gather.2.cloned.1.call-done = bf16[4,64,3072]{2,1,0:T(8,128)(2,1)} async-done(((bf16[4,64,768]{2,1,0:T(8,128)(2,1)}), bf16[4,64,3072]{2,1,0:T(8,128)(2,1)}) %all-gather.2.cloned.1.call-update) | async-done | bytes 1572880 | tf_op jit(solution)/shard_map/while/body/eval_jaxpr/all_gather | solution.py:70
  337.8 9.9 %fusion.123 = (f32[4,64]{1,0:T(4,128)}, f32[4,64,2048]{2,1,0:T(8,128)S(1)}) fusion(bf16[1,2,4,64,2048]{4,3,2,1,0:T(8,128)(2,1)S(1)} %copy-done.5, s32[]{:T(128)S(6)} %min.13, bf16[1,2,4,64,2048]{4,3,2,1,0:T(8,128)(2,1)} %get-tuple-element.699, bf16[4,64,3072]{2,1,0:T(8,128)(2,1)} %all-gather.2.cloned.1.call-done, ...), kind=kOutput, calls=%fused_computation.17.clone.1 | convolution fusion | flops 3225943808 | bytes 18351108 | tf_op jit(solution)/shard_map/while/body/eval_jaxpr/scw,fw->scf/dot_general | solution.py:39
  347.7 10.7 %fusion.129 = f32[4,64,3072]{2,1,0:T(8,128)} fusion(bf16[3072,2048]{1,0:T(8,128)(2,1)} %get-tuple-element.701, f32[4,64,2048]{2,1,0:T(8,128)S(1)} %get-tuple-element.640, bf16[1,2,4,64,2048]{4,3,2,1,0:T(8,128)(2,1)S(1)} %copy-done.6, s32[]{:T(128)S(6)} %min.13), kind=kOutput, calls=%fused_computation.2.clone.1 | convolution fusion | flops 3224895488 | bytes 18874372 | tf_op jit(solution)/shard_map/while/body/eval_jaxpr/scf,df->scd/dot_general | solution.py:80
  358.4 11.6 %fusion.130 = f32[4,64,3072]{2,1,0:T(8,128)} fusion(f32[4,64,3072]{2,1,0:T(8,128)} %fusion.129, bf16[3072,2048]{1,0:T(8,128)(2,1)} %get-tuple-element.700, f32[4,64,2048]{2,1,0:T(8,128)} %copy-done.7, bf16[1,2,4,64,2048]{4,3,2,1,0:T(8,128)(2,1)S(1)} %copy-done.6, s32[]{:T(128)S(6)} %min.13, bf16[1,2,4,64,2048]{4,3,2,1,0:T(8,128)(2,1)S(1)} %copy-done.5), kind=kOutput, calls=%fused_computation.8.clone.1 | convolution fusion | flops 3228303360 | bytes 23068676 | tf_op jit(solution)/shard_map/while/body/eval_jaxpr/scf,df->scd/dot_general | solution.py:79
  371.1 5.9 %psum.62 = f32[80]{0:T(128)S(1)} all-reduce(f32[80]{0:T(128)S(1)} %fusion.125), channel_id=1, replica_groups=mesh['section'=2,'expert'=4,'tensor'=4] {'tensor'}, use_global_device_ids=true, to_apply=%region_2.2 | all-reduce | flops 80 | bytes 640 | tf_op jit(solution)/shard_map/while/body/eval_jaxpr/psum | solution.py:43
  377.2 4.8 %all-to-all-start.1 = ((f32[4,1,64]{2,1,0:T(1,128)}), f32[4,1,64]{2,1,0:T(1,128)S(1)}, u32[]{:S(2)}, u32[]{:S(2)}) async-start(f32[4,1,64]{2,1,0:T(1,128)} %bitcast.160), calls=%async_computation.1 | async-start | bytes 4096 | tf_op jit(solution)/shard_map/while/body/eval_jaxpr/all_to_all | solution.py:85
  382.0 5.5 %all-to-all-done.1 = f32[4,1,64]{2,1,0:T(1,128)S(1)} async-done(((f32[4,1,64]{2,1,0:T(1,128)}), f32[4,1,64]{2,1,0:T(1,128)S(1)}, u32[]{:S(2)}, u32[]{:S(2)}) %all-to-all-start.1) | async-done | bytes 1056 | tf_op jit(solution)/shard_map/while/body/eval_jaxpr/all_to_all | solution.py:85
  387.5 20.5 %reduce-scatter.2.cloned.1.call-done = f32[4,64,768]{2,1,0:T(8,128)} async-done(((f32[4,64,3072]{2,1,0:T(8,128)}), f32[4,64,768]{2,1,0:T(8,128)}) %reduce-scatter.2.cloned.1.call-update) | async-done | bytes 786448 | tf_op jit(solution)/shard_map/while/body/eval_jaxpr/reduce_scatter | solution.py:82
  407.9 4.6 %all-to-all-start.2 = ((f32[4,64,768]{2,1,0:T(8,128)}), f32[4,64,768]{2,1,0:T(8,128)S(1)}, u32[]{:S(2)}, u32[]{:S(2)}) async-start(f32[4,64,768]{2,1,0:T(8,128)} %reduce-scatter.2.cloned.1.call-done), calls=%async_computation.3 | async-start | bytes 1572864 | tf_op jit(solution)/shard_map/while/body/eval_jaxpr/all_to_all | solution.py:84
  414.1 6.0 %all-reduce.3 = (f32[80,2]{0,1:T(2,128)S(1)}, f32[80,4]{0,1:T(4,128)S(1)}) all-reduce(f32[80,2]{0,1:T(2,128)S(1)} %bitcast.172, f32[80,4]{0,1:T(4,128)S(1)} %fusion.126), channel_id=1, replica_groups=mesh['section'=2,'expert'=4,'tensor'=4] {'tensor'}, use_global_device_ids=true, to_apply=%region_11.11 | all-reduce | flops 480 | bytes 3840 | tf_op jit(solution)/shard_map/while/body/eval_jaxpr/psum | solution.py:97
  420.5 12.0 %all-to-all-done.2 = f32[4,64,768]{2,1,0:T(8,128)S(1)} async-done(((f32[4,64,768]{2,1,0:T(8,128)}), f32[4,64,768]{2,1,0:T(8,128)S(1)}, u32[]{:S(2)}, u32[]{:S(2)}) %all-to-all-start.2) | async-done | bytes 786464 | tf_op jit(solution)/shard_map/while/body/eval_jaxpr/all_to_all | solution.py:84
  433.2 5.9 %psum.63 = f32[80]{0:T(128)S(1)} all-reduce(f32[80]{0:T(128)S(1)} %get-tuple-element.643), channel_id=1, replica_groups=mesh['section'=2,'expert'=4,'tensor'=4] {'tensor'}, use_global_device_ids=true, to_apply=%region_13.13 | all-reduce | flops 80 | bytes 640 | tf_op jit(solution)/shard_map/while/body/eval_jaxpr/psum | solution.py:104
  439.3 1.3 collective-permute-start
  440.6 5.5 %collective-permute-done = bf16[80,768]{1,0:T(8,128)(2,1)S(1)} collective-permute-done((bf16[80,768]{1,0:T(8,128)(2,1)S(1)}, bf16[80,768]{1,0:T(8,128)(2,1)S(1)}, u32[]{:S(2)}, u32[]{:S(2)}) %collective-permute-start) | collective-permute-done | bytes 122912 | tf_op jit(solution)/shard_map/while/body/eval_jaxpr/ppermute | solution.py:13
  (168 shorter events, 26.2 us)
Async XLA Ops:
  7.3 41.9 %copy-start.5 = (bf16[1,2,4,64,2048]{4,3,2,1,0:T(8,128)(2,1)S(1)}, bf16[1,2,4,64,2048]{4,3,2,1,0:T(8,128)(2,1)}, u32[]{:S(2)}) copy-start(bf16[1,2,4,64,2048]{4,3,2,1,0:T(8,128)(2,1)} %get-tuple-element.698) | copy-start | bytes 6291460 | tf_op jit(solution)/shard_map/while
  7.3 41.9 %all-gather.2.cloned.1.call-start = ((), (), s32[]{:S(2)}) async-start(), calls=%async_computation.4 | async-start | bytes 1966080 | tf_op jit(solution)/shard_map/while/body/eval_jaxpr/all_gather | solution.py:70
  30.3 89.0 %reduce-scatter.2.cloned.1.call-start = ((), (), s32[]{:S(2)}) async-start(), calls=%async_computation.5 | async-start | bytes 3932160 | tf_op jit(solution)/shard_map/while/body/eval_jaxpr/reduce_scatter | solution.py:82
  49.2 9.9 %copy-start.6 = (bf16[1,2,4,64,2048]{4,3,2,1,0:T(8,128)(2,1)S(1)}, bf16[1,2,4,64,2048]{4,3,2,1,0:T(8,128)(2,1)}, u32[]{:S(2)}) copy-start(bf16[1,2,4,64,2048]{4,3,2,1,0:T(8,128)(2,1)} %get-tuple-element.699) | copy-start | bytes 6291460 | tf_op jit(solution)/shard_map/while
  59.1 10.7 %copy-start.7 = (f32[4,64,2048]{2,1,0:T(8,128)}, f32[4,64,2048]{2,1,0:T(8,128)S(1)}, u32[]{:S(2)}) copy-start(f32[4,64,2048]{2,1,0:T(8,128)S(1)} %get-tuple-element.640) | copy-start | bytes 6291460 | tf_op jit(solution)/shard_map/while
  81.4 0.9 copy-start
  81.4 7.0 %copy-start.3 = (bf16[768,4]{0,1:T(4,128)(2,1)S(1)}, bf16[768,4]{0,1:T(4,128)(2,1)}, u32[]{:S(2)}) copy-start(bf16[768,4]{0,1:T(4,128)(2,1)} %get-tuple-element.696) | copy-start | bytes 18436 | tf_op jit(solution)/shard_map/while
  81.4 11.9 %copy-start.4 = (s32[1,2,80,2]{2,3,1,0:T(2,128)S(1)}, s32[1,2,80,2]{2,3,1,0:T(2,128)}, u32[]{:S(2)}) copy-start(s32[1,2,80,2]{2,3,1,0:T(2,128)} %get-tuple-element.694) | copy-start | bytes 3844 | tf_op jit(solution)/shard_map/while
  81.4 69.1 %copy-start.1 = (bf16[2,80,768]{2,1,0:T(8,128)(2,1)S(1)}, bf16[2,80,768]{2,1,0:T(8,128)(2,1)}, u32[]{:S(2)}) copy-start(bf16[2,80,768]{2,1,0:T(8,128)(2,1)} %get-tuple-element.692) | copy-start | bytes 737284 | tf_op jit(solution)/shard_map/while
  88.6 10.3 %all-to-all-start.1 = ((f32[4,1,64]{2,1,0:T(1,128)}), f32[4,1,64]{2,1,0:T(1,128)S(1)}, u32[]{:S(2)}, u32[]{:S(2)}) async-start(f32[4,1,64]{2,1,0:T(1,128)} %bitcast.160), calls=%async_computation.1 | async-start | bytes 4096 | tf_op jit(solution)/shard_map/while/body/eval_jaxpr/all_to_all | solution.py:85
  119.3 24.5 %all-to-all-start.2 = ((f32[4,64,768]{2,1,0:T(8,128)}), f32[4,64,768]{2,1,0:T(8,128)S(1)}, u32[]{:S(2)}, u32[]{:S(2)}) async-start(f32[4,64,768]{2,1,0:T(8,128)} %reduce-scatter.2.cloned.1.call-done), calls=%async_computation.3 | async-start | bytes 1572864 | tf_op jit(solution)/shard_map/while/body/eval_jaxpr/all_to_all | solution.py:84
  150.7 6.8 %collective-permute-start = (bf16[80,768]{1,0:T(8,128)(2,1)S(1)}, bf16[80,768]{1,0:T(8,128)(2,1)S(1)}, u32[]{:S(2)}, u32[]{:S(2)}) collective-permute-start(bf16[80,768]{1,0:T(8,128)(2,1)S(1)} %get-tuple-element.645), channel_id=1, source_target_pairs={{16,0},{17,1},{18,2},{19,3},{20,4},{21,5},{22,6},{23,7},{24,8},{25... | collective-permute-start | bytes 368648 | tf_op jit(solution)/shard_map/while/body/eval_jaxpr/ppermute | solution.py:13
  157.5 36.0 %copy-start.5 = (bf16[1,2,4,64,2048]{4,3,2,1,0:T(8,128)(2,1)S(1)}, bf16[1,2,4,64,2048]{4,3,2,1,0:T(8,128)(2,1)}, u32[]{:S(2)}) copy-start(bf16[1,2,4,64,2048]{4,3,2,1,0:T(8,128)(2,1)} %get-tuple-element.698) | copy-start | bytes 6291460 | tf_op jit(solution)/shard_map/while
  157.5 36.0 %all-gather.2.cloned.1.call-start = ((), (), s32[]{:S(2)}) async-start(), calls=%async_computation.4 | async-start | bytes 1966080 | tf_op jit(solution)/shard_map/while/body/eval_jaxpr/all_gather | solution.py:70
  176.1 87.5 %reduce-scatter.2.cloned.1.call-start = ((), (), s32[]{:S(2)}) async-start(), calls=%async_computation.5 | async-start | bytes 3932160 | tf_op jit(solution)/shard_map/while/body/eval_jaxpr/reduce_scatter | solution.py:82
  193.5 9.9 %copy-start.6 = (bf16[1,2,4,64,2048]{4,3,2,1,0:T(8,128)(2,1)S(1)}, bf16[1,2,4,64,2048]{4,3,2,1,0:T(8,128)(2,1)}, u32[]{:S(2)}) copy-start(bf16[1,2,4,64,2048]{4,3,2,1,0:T(8,128)(2,1)} %get-tuple-element.699) | copy-start | bytes 6291460 | tf_op jit(solution)/shard_map/while
  203.3 10.7 %copy-start.7 = (f32[4,64,2048]{2,1,0:T(8,128)}, f32[4,64,2048]{2,1,0:T(8,128)S(1)}, u32[]{:S(2)}) copy-start(f32[4,64,2048]{2,1,0:T(8,128)S(1)} %get-tuple-element.640) | copy-start | bytes 6291460 | tf_op jit(solution)/shard_map/while
  225.7 0.9 copy-start
  225.7 6.9 %copy-start.3 = (bf16[768,4]{0,1:T(4,128)(2,1)S(1)}, bf16[768,4]{0,1:T(4,128)(2,1)}, u32[]{:S(2)}) copy-start(bf16[768,4]{0,1:T(4,128)(2,1)} %get-tuple-element.696) | copy-start | bytes 18436 | tf_op jit(solution)/shard_map/while
  225.7 11.9 %copy-start.4 = (s32[1,2,80,2]{2,3,1,0:T(2,128)S(1)}, s32[1,2,80,2]{2,3,1,0:T(2,128)}, u32[]{:S(2)}) copy-start(s32[1,2,80,2]{2,3,1,0:T(2,128)} %get-tuple-element.694) | copy-start | bytes 3844 | tf_op jit(solution)/shard_map/while
  225.7 69.1 %copy-start.1 = (bf16[2,80,768]{2,1,0:T(8,128)(2,1)S(1)}, bf16[2,80,768]{2,1,0:T(8,128)(2,1)}, u32[]{:S(2)}) copy-start(bf16[2,80,768]{2,1,0:T(8,128)(2,1)} %get-tuple-element.692) | copy-start | bytes 737284 | tf_op jit(solution)/shard_map/while
  232.8 10.3 %all-to-all-start.1 = ((f32[4,1,64]{2,1,0:T(1,128)}), f32[4,1,64]{2,1,0:T(1,128)S(1)}, u32[]{:S(2)}, u32[]{:S(2)}) async-start(f32[4,1,64]{2,1,0:T(1,128)} %bitcast.160), calls=%async_computation.1 | async-start | bytes 4096 | tf_op jit(solution)/shard_map/while/body/eval_jaxpr/all_to_all | solution.py:85
  263.6 24.5 %all-to-all-start.2 = ((f32[4,64,768]{2,1,0:T(8,128)}), f32[4,64,768]{2,1,0:T(8,128)S(1)}, u32[]{:S(2)}, u32[]{:S(2)}) async-start(f32[4,64,768]{2,1,0:T(8,128)} %reduce-scatter.2.cloned.1.call-done), calls=%async_computation.3 | async-start | bytes 1572864 | tf_op jit(solution)/shard_map/while/body/eval_jaxpr/all_to_all | solution.py:84
  295.0 6.8 %collective-permute-start = (bf16[80,768]{1,0:T(8,128)(2,1)S(1)}, bf16[80,768]{1,0:T(8,128)(2,1)S(1)}, u32[]{:S(2)}, u32[]{:S(2)}) collective-permute-start(bf16[80,768]{1,0:T(8,128)(2,1)S(1)} %get-tuple-element.645), channel_id=1, source_target_pairs={{16,0},{17,1},{18,2},{19,3},{20,4},{21,5},{22,6},{23,7},{24,8},{25... | collective-permute-start | bytes 368648 | tf_op jit(solution)/shard_map/while/body/eval_jaxpr/ppermute | solution.py:13
  301.8 36.0 %copy-start.5 = (bf16[1,2,4,64,2048]{4,3,2,1,0:T(8,128)(2,1)S(1)}, bf16[1,2,4,64,2048]{4,3,2,1,0:T(8,128)(2,1)}, u32[]{:S(2)}) copy-start(bf16[1,2,4,64,2048]{4,3,2,1,0:T(8,128)(2,1)} %get-tuple-element.698) | copy-start | bytes 6291460 | tf_op jit(solution)/shard_map/while
  301.8 36.0 %all-gather.2.cloned.1.call-start = ((), (), s32[]{:S(2)}) async-start(), calls=%async_computation.4 | async-start | bytes 1966080 | tf_op jit(solution)/shard_map/while/body/eval_jaxpr/all_gather | solution.py:70
  320.4 87.5 %reduce-scatter.2.cloned.1.call-start = ((), (), s32[]{:S(2)}) async-start(), calls=%async_computation.5 | async-start | bytes 3932160 | tf_op jit(solution)/shard_map/while/body/eval_jaxpr/reduce_scatter | solution.py:82
  337.8 9.9 %copy-start.6 = (bf16[1,2,4,64,2048]{4,3,2,1,0:T(8,128)(2,1)S(1)}, bf16[1,2,4,64,2048]{4,3,2,1,0:T(8,128)(2,1)}, u32[]{:S(2)}) copy-start(bf16[1,2,4,64,2048]{4,3,2,1,0:T(8,128)(2,1)} %get-tuple-element.699) | copy-start | bytes 6291460 | tf_op jit(solution)/shard_map/while
  347.7 10.7 %copy-start.7 = (f32[4,64,2048]{2,1,0:T(8,128)}, f32[4,64,2048]{2,1,0:T(8,128)S(1)}, u32[]{:S(2)}) copy-start(f32[4,64,2048]{2,1,0:T(8,128)S(1)} %get-tuple-element.640) | copy-start | bytes 6291460 | tf_op jit(solution)/shard_map/while
  370.0 0.9 copy-start
  370.0 7.0 %copy-start.3 = (bf16[768,4]{0,1:T(4,128)(2,1)S(1)}, bf16[768,4]{0,1:T(4,128)(2,1)}, u32[]{:S(2)}) copy-start(bf16[768,4]{0,1:T(4,128)(2,1)} %get-tuple-element.696) | copy-start | bytes 18436 | tf_op jit(solution)/shard_map/while
  370.0 11.9 %copy-start.4 = (s32[1,2,80,2]{2,3,1,0:T(2,128)S(1)}, s32[1,2,80,2]{2,3,1,0:T(2,128)}, u32[]{:S(2)}) copy-start(s32[1,2,80,2]{2,3,1,0:T(2,128)} %get-tuple-element.694) | copy-start | bytes 3844 | tf_op jit(solution)/shard_map/while
  370.0 69.1 %copy-start.1 = (bf16[2,80,768]{2,1,0:T(8,128)(2,1)S(1)}, bf16[2,80,768]{2,1,0:T(8,128)(2,1)}, u32[]{:S(2)}) copy-start(bf16[2,80,768]{2,1,0:T(8,128)(2,1)} %get-tuple-element.692) | copy-start | bytes 737284 | tf_op jit(solution)/shard_map/while
  377.2 10.3 %all-to-all-start.1 = ((f32[4,1,64]{2,1,0:T(1,128)}), f32[4,1,64]{2,1,0:T(1,128)S(1)}, u32[]{:S(2)}, u32[]{:S(2)}) async-start(f32[4,1,64]{2,1,0:T(1,128)} %bitcast.160), calls=%async_computation.1 | async-start | bytes 4096 | tf_op jit(solution)/shard_map/while/body/eval_jaxpr/all_to_all | solution.py:85
  407.9 24.5 %all-to-all-start.2 = ((f32[4,64,768]{2,1,0:T(8,128)}), f32[4,64,768]{2,1,0:T(8,128)S(1)}, u32[]{:S(2)}, u32[]{:S(2)}) async-start(f32[4,64,768]{2,1,0:T(8,128)} %reduce-scatter.2.cloned.1.call-done), calls=%async_computation.3 | async-start | bytes 1572864 | tf_op jit(solution)/shard_map/while/body/eval_jaxpr/all_to_all | solution.py:84
  439.3 6.8 %collective-permute-start = (bf16[80,768]{1,0:T(8,128)(2,1)S(1)}, bf16[80,768]{1,0:T(8,128)(2,1)S(1)}, u32[]{:S(2)}, u32[]{:S(2)}) collective-permute-start(bf16[80,768]{1,0:T(8,128)(2,1)S(1)} %get-tuple-element.645), channel_id=1, source_target_pairs={{16,0},{17,1},{18,2},{19,3},{20,4},{21,5},{22,6},{23,7},{24,8},{25... | collective-permute-start | bytes 368648 | tf_op jit(solution)/shard_map/while/body/eval_jaxpr/ppermute | solution.py:13
  446.1 0.7 copy-start.2
Sparse Core Ops, SparseCore 0:
  30.4 18.7 all-gather.1
  81.6 37.7 reduce-scatter.1
  176.2 17.1 all-gather.1
  225.8 37.7 reduce-scatter.1
  320.5 17.2 all-gather.1
  370.2 37.7 reduce-scatter.1
where the time goes:
time: 455 us; the launch traced here: 454 us
  waiting for transfers between devices  184 us (40%)
  matrix products  105 us (23%)
  blocking collectives  98.8 us (22%)
  starting transfers between devices  32.2 us (7%)
  between operations  13.4 us (3%)
  other arithmetic  10.5 us (2%)
  local copies, waits for them, and re-layouts  10 us (2%)
    reduce_scatter x3, waiting for transfers between devices, layer_back(): lax.psum_scatter(unit, 'tensor', scatter_dimension=2, tiled=True)  61.5 us
    all_gather x3, waiting for transfers between devices, layer_back(): lax.all_gather(arrived, 'tensor', axis=2, tiled=True)  53.5 us
    all_to_all x3, blocking collectives, layer_back(): lax.all_to_all(copies, 'expert', split_axis=0, concat_axis=0, tiled=True)  45.2 us
    all_to_all x3, waiting for transfers between devices, layer_back(): lax.all_to_all(unit_share, 'expert', split_axis=0, concat_axis=0, tiled=T...  35.9 us
    dot_general x3, matrix products, layer_back(): jnp.einsum('scf,df->scd', gate_grad, gate_mat, preferred_element_type=jnp...  34.9 us
    dot_general x3, matrix products, layer_back(): jnp.einsum('scf,df->scd', up_grad, up_mat, preferred_element_type=jnp.flo...  32.1 us
    dot_general x3, matrix products, add_columns(): jnp.einsum('scw,fw->scf', piece, down_mat, preferred_element_type=jnp.flo...  29.6 us
    psum x3, blocking collectives, layer_back(): prob_grad = lax.psum(prob_part, 'tensor')  18.1 us
  transfers between devices with their start and end apart: 15, of which 15 were waited for; matrix products, arithmetic and copies ran while one was open for 1% of the time, Pallas kernels for 0%

commit v1 on v0

--- a/solution.py
+++ b/solution.py
@@ -67,7 +67,11 @@
             (experts, group, capacity, quarter),
         ).reshape(holders, capacity, quarter)
         arrived = lax.all_to_all(copies, "expert", split_axis=0, concat_axis=0, tiled=True)
-        back_act = add_columns(lax.all_gather(arrived, "tensor", axis=2, tiled=True))
+
+        def _match_stocks(x_part):
+            return jnp.concatenate(jax.lax.all_gather(x_part, "tensor"), axis=2)
+
+        back_act = add_columns(_match_stocks(arrived))
         gate_act = gate_saved.astype(jnp.float32)
         up_act = up_saved.astype(jnp.float32)
         sigma = jax.nn.sigmoid(gate_act)

time: 455 us -> 465 us (1.022)
  local copies, waits for them, and re-layouts: 10 us -> 21 us
    all_gather x0 -> x3, local copies, waits for them, and re-layouts: none -> 7.87 us  [_match_stocks(): return jnp.concatenate(jax.lax.all_gather(x_part, 'tensor'), axis=2)]
where the time goes in v1:
time: 465 us; the launch traced here: 464 us
  waiting for transfers between devices  184 us (40%)
  matrix products  104 us (22%)
  blocking collectives  98.8 us (21%)
  starting transfers between devices  32.2 us (7%)
  local copies, waits for them, and re-layouts  21 us (5%)
  between operations  13.4 us (3%)
  other arithmetic  10.5 us (2%)
    reduce_scatter x3, waiting for transfers between devices, layer_back(): lax.psum_scatter(unit, 'tensor', scatter_dimension=2, tiled=True)  61.5 us
    all_gather x3, waiting for transfers between devices, _match_stocks(): return jnp.concatenate(jax.lax.all_gather(x_part, 'tensor'), axis=2)  53.4 us
    all_to_all x3, blocking collectives, layer_back(): lax.all_to_all(copies, 'expert', split_axis=0, concat_axis=0, tiled=True)  45.2 us
    all_to_all x3, waiting for transfers between devices, layer_back(): lax.all_to_all(unit_share, 'expert', split_axis=0, concat_axis=0, tiled=T...  35.9 us
    dot_general x3, matrix products, layer_back(): jnp.einsum('scf,df->scd', gate_grad, gate_mat, preferred_element_type=jnp...  34.9 us
    dot_general x3, matrix products, layer_back(): jnp.einsum('scf,df->scd', up_grad, up_mat, preferred_element_type=jnp.flo...  32.2 us
    dot_general x3, matrix products, add_columns(): jnp.einsum('scw,fw->scf', piece, down_mat, preferred_element_type=jnp.flo...  29.1 us
    psum x3, blocking collectives, layer_back(): prob_grad = lax.psum(prob_part, 'tensor')  18.1 us
  transfers between devices with their start and end apart: 15, of which 15 were waited for; matrix products, arithmetic and copies ran while one was open for 1% of the time, Pallas kernels for 0%

profile of v1, /device:TPU:0, one launch (start us, length us, event | category | flops | bytes accessed | tf_op | source)
XLA Modules:
  0.0 464.3 jit_solution(16338299104533568551)
XLA Ops:
  7.3 449.4 %while.19 = (s32[]{:T(128)}, bf16[80,768]{1,0:T(8,128)(2,1)S(1)}, bf16[2,80,768]{2,1,0:T(8,128)(2,1)S(1)}, s32[]{:T(128)}, pred[]{:T(512)}, /*index=5*/bf16[2,80...) while((s32[]{:T(128)}, bf16[80,768]{1,0:T(8,128)(2,1)S(1)}, ...), condition=%wide.region_14.15_spmd.clone.clone, body=%wide.region_0.14_spmd.clone.clone.sunk | while | flops 9905498112 | bytes 127502008 | solution.py:136
  12.2 17.9 %all_to_all.47 = bf16[4,64,768]{2,1,0:T(8,128)(2,1)} all-to-all(bf16[4,64,768]{2,1,0:T(8,128)(2,1)S(1)} %bitcast.176), channel_id=1, replica_groups=mesh['section'=2,'expert'=4,'tensor'=4] {'expert'}, dimensions={0} | all-to-all | bytes 786432 | tf_op jit(solution)/shard_map/while/body/eval_jaxpr/all_to_all | solution.py:69
  30.2 18.9 %all-gather.6.cloned.1.call-done = bf16[16,64,768]{2,1,0:T(8,128)(2,1)} async-done(((bf16[4,64,768]{2,1,0:T(8,128)(2,1)}), bf16[16,64,768]{2,1,0:T(8,128)(2,1)}) %all-gather.6.cloned.1.call-update) | async-done | bytes 1572880 | tf_op jit(solution)/shard_map/while/body/eval_jaxpr/all_gather | solution.py:72
  49.0 2.6 copy.55
  52.9 9.7 %fusion.123 = (f32[4,64]{1,0:T(4,128)}, f32[4,64,2048]{2,1,0:T(8,128)S(1)}) fusion(bf16[1,2,4,64,2048]{4,3,2,1,0:T(8,128)(2,1)} %get-tuple-element.698, s32[]{:T(128)S(6)} %min.13, bf16[1,2,4,64,2048]{4,3,2,1,0:T(8,128)(2,1)} %get-tuple-element.699, bf16[4,64,3072]{2,1,0:T(8,128)(2,1)S(1)} %reshape.314, bf16[2048,3072]{1,0:T(8,128)(2,1)} %get-tuple-element.697), kind=kOutput, calls=%fused_computation.17.clone.1 | convolution fusion | flops 3225943808 | bytes 18351108 | tf_op jit(solution)/shard_map/while/body/eval_jaxpr/scw,fw->scf/dot_general | solution.py:39
  62.6 10.7 %fusion.129 = f32[4,64,3072]{2,1,0:T(8,128)} fusion(bf16[3072,2048]{1,0:T(8,128)(2,1)} %get-tuple-element.701, f32[4,64,2048]{2,1,0:T(8,128)S(1)} %get-tuple-element.640, bf16[1,2,4,64,2048]{4,3,2,1,0:T(8,128)(2,1)S(1)} %copy-done.6, s32[]{:T(128)S(6)} %min.13), kind=kOutput, calls=%fused_computation.2.clone.1 | convolution fusion | flops 3224895488 | bytes 18874372 | tf_op jit(solution)/shard_map/while/body/eval_jaxpr/scf,df->scd/dot_general | solution.py:84
  73.3 11.6 %fusion.130 = f32[4,64,3072]{2,1,0:T(8,128)} fusion(f32[4,64,3072]{2,1,0:T(8,128)} %fusion.129, bf16[3072,2048]{1,0:T(8,128)(2,1)} %get-tuple-element.700, f32[4,64,2048]{2,1,0:T(8,128)} %copy-done.8, bf16[1,2,4,64,2048]{4,3,2,1,0:T(8,128)(2,1)S(1)} %copy-done.7, s32[]{:T(128)S(6)} %min.13, bf16[1,2,4,64,2048]{4,3,2,1,0:T(8,128)(2,1)S(1)} %copy-done.5), kind=kOutput, calls=%fused_computation.8.clone.1 | convolution fusion | flops 3228303360 | bytes 23068676 | tf_op jit(solution)/shard_map/while/body/eval_jaxpr/scf,df->scd/dot_general | solution.py:83
  86.0 5.9 %psum.62 = f32[80]{0:T(128)S(1)} all-reduce(f32[80]{0:T(128)S(1)} %fusion.125), channel_id=1, replica_groups=mesh['section'=2,'expert'=4,'tensor'=4] {'tensor'}, use_global_device_ids=true, to_apply=%region_2.2 | all-reduce | flops 80 | bytes 640 | tf_op jit(solution)/shard_map/while/body/eval_jaxpr/psum | solution.py:43
  92.1 4.8 %all-to-all-start.1 = ((f32[4,1,64]{2,1,0:T(1,128)}), f32[4,1,64]{2,1,0:T(1,128)S(1)}, u32[]{:S(2)}, u32[]{:S(2)}) async-start(f32[4,1,64]{2,1,0:T(1,128)} %bitcast.168), calls=%async_computation.1 | async-start | bytes 4096 | tf_op jit(solution)/shard_map/while/body/eval_jaxpr/all_to_all | solution.py:89
  96.9 5.5 %all-to-all-done.1 = f32[4,1,64]{2,1,0:T(1,128)S(1)} async-done(((f32[4,1,64]{2,1,0:T(1,128)}), f32[4,1,64]{2,1,0:T(1,128)S(1)}, u32[]{:S(2)}, u32[]{:S(2)}) %all-to-all-start.1) | async-done | bytes 1056 | tf_op jit(solution)/shard_map/while/body/eval_jaxpr/all_to_all | solution.py:89
  102.4 20.5 %reduce-scatter.2.cloned.1.call-done = f32[4,64,768]{2,1,0:T(8,128)} async-done(((f32[4,64,3072]{2,1,0:T(8,128)}), f32[4,64,768]{2,1,0:T(8,128)}) %reduce-scatter.2.cloned.1.call-update) | async-done | bytes 786448 | tf_op jit(solution)/shard_map/while/body/eval_jaxpr/reduce_scatter | solution.py:86
  122.9 4.6 all-to-all-start.2
  129.1 6.0 %all-reduce.3 = (f32[80,2]{0,1:T(2,128)S(1)}, f32[80,4]{0,1:T(4,128)S(1)}) all-reduce(f32[80,2]{0,1:T(2,128)S(1)} %bitcast.182, f32[80,4]{0,1:T(4,128)S(1)} %fusion.126), channel_id=1, replica_groups=mesh['section'=2,'expert'=4,'tensor'=4] {'tensor'}, use_global_device_ids=true, to_apply=%region_11.11 | all-reduce | flops 480 | bytes 3840 | tf_op jit(solution)/shard_map/while/body/eval_jaxpr/psum | solution.py:101
  135.5 12.0 %all-to-all-done.2 = f32[4,64,768]{2,1,0:T(8,128)S(1)} async-done(((f32[4,64,768]{2,1,0:T(8,128)}), f32[4,64,768]{2,1,0:T(8,128)S(1)}, u32[]{:S(2)}, u32[]{:S(2)}) %all-to-all-start.2) | async-done | bytes 786464 | tf_op jit(solution)/shard_map/while/body/eval_jaxpr/all_to_all | solution.py:88
  148.2 5.9 %psum.63 = f32[80]{0:T(128)S(1)} all-reduce(f32[80]{0:T(128)S(1)} %get-tuple-element.643), channel_id=1, replica_groups=mesh['section'=2,'expert'=4,'tensor'=4] {'tensor'}, use_global_device_ids=true, to_apply=%region_13.13 | all-reduce | flops 80 | bytes 640 | tf_op jit(solution)/shard_map/while/body/eval_jaxpr/psum | solution.py:108
  154.3 1.3 collective-permute-start
  155.6 5.5 %collective-permute-done = bf16[80,768]{1,0:T(8,128)(2,1)S(1)} collective-permute-done((bf16[80,768]{1,0:T(8,128)(2,1)S(1)}, bf16[80,768]{1,0:T(8,128)(2,1)S(1)}, u32[]{:S(2)}, u32[]{:S(2)}) %collective-permute-start) | collective-permute-done | bytes 122912 | tf_op jit(solution)/shard_map/while/body/eval_jaxpr/ppermute | solution.py:13
  165.9 13.6 %all_to_all.47 = bf16[4,64,768]{2,1,0:T(8,128)(2,1)} all-to-all(bf16[4,64,768]{2,1,0:T(8,128)(2,1)S(1)} %bitcast.176), channel_id=1, replica_groups=mesh['section'=2,'expert'=4,'tensor'=4] {'expert'}, dimensions={0} | all-to-all | bytes 786432 | tf_op jit(solution)/shard_map/while/body/eval_jaxpr/all_to_all | solution.py:69
  179.6 17.3 %all-gather.6.cloned.1.call-done = bf16[16,64,768]{2,1,0:T(8,128)(2,1)} async-done(((bf16[4,64,768]{2,1,0:T(8,128)(2,1)}), bf16[16,64,768]{2,1,0:T(8,128)(2,1)}) %all-gather.6.cloned.1.call-update) | async-done | bytes 1572880 | tf_op jit(solution)/shard_map/while/body/eval_jaxpr/all_gather | solution.py:72
  196.9 2.6 copy.55
  200.7 9.7 %fusion.123 = (f32[4,64]{1,0:T(4,128)}, f32[4,64,2048]{2,1,0:T(8,128)S(1)}) fusion(bf16[1,2,4,64,2048]{4,3,2,1,0:T(8,128)(2,1)} %get-tuple-element.698, s32[]{:T(128)S(6)} %min.13, bf16[1,2,4,64,2048]{4,3,2,1,0:T(8,128)(2,1)} %get-tuple-element.699, bf16[4,64,3072]{2,1,0:T(8,128)(2,1)S(1)} %reshape.314, bf16[2048,3072]{1,0:T(8,128)(2,1)} %get-tuple-element.697), kind=kOutput, calls=%fused_computation.17.clone.1 | convolution fusion | flops 3225943808 | bytes 18351108 | tf_op jit(solution)/shard_map/while/body/eval_jaxpr/scw,fw->scf/dot_general | solution.py:39
  210.4 10.7 %fusion.129 = f32[4,64,3072]{2,1,0:T(8,128)} fusion(bf16[3072,2048]{1,0:T(8,128)(2,1)} %get-tuple-element.701, f32[4,64,2048]{2,1,0:T(8,128)S(1)} %get-tuple-element.640, bf16[1,2,4,64,2048]{4,3,2,1,0:T(8,128)(2,1)S(1)} %copy-done.6, s32[]{:T(128)S(6)} %min.13), kind=kOutput, calls=%fused_computation.2.clone.1 | convolution fusion | flops 3224895488 | bytes 18874372 | tf_op jit(solution)/shard_map/while/body/eval_jaxpr/scf,df->scd/dot_general | solution.py:84
  221.2 11.6 %fusion.130 = f32[4,64,3072]{2,1,0:T(8,128)} fusion(f32[4,64,3072]{2,1,0:T(8,128)} %fusion.129, bf16[3072,2048]{1,0:T(8,128)(2,1)} %get-tuple-element.700, f32[4,64,2048]{2,1,0:T(8,128)} %copy-done.8, bf16[1,2,4,64,2048]{4,3,2,1,0:T(8,128)(2,1)S(1)} %copy-done.7, s32[]{:T(128)S(6)} %min.13, bf16[1,2,4,64,2048]{4,3,2,1,0:T(8,128)(2,1)S(1)} %copy-done.5), kind=kOutput, calls=%fused_computation.8.clone.1 | convolution fusion | flops 3228303360 | bytes 23068676 | tf_op jit(solution)/shard_map/while/body/eval_jaxpr/scf,df->scd/dot_general | solution.py:83
  233.9 5.9 %psum.62 = f32[80]{0:T(128)S(1)} all-reduce(f32[80]{0:T(128)S(1)} %fusion.125), channel_id=1, replica_groups=mesh['section'=2,'expert'=4,'tensor'=4] {'tensor'}, use_global_device_ids=true, to_apply=%region_2.2 | all-reduce | flops 80 | bytes 640 | tf_op jit(solution)/shard_map/while/body/eval_jaxpr/psum | solution.py:43
  240.0 4.8 %all-to-all-start.1 = ((f32[4,1,64]{2,1,0:T(1,128)}), f32[4,1,64]{2,1,0:T(1,128)S(1)}, u32[]{:S(2)}, u32[]{:S(2)}) async-start(f32[4,1,64]{2,1,0:T(1,128)} %bitcast.168), calls=%async_computation.1 | async-start | bytes 4096 | tf_op jit(solution)/shard_map/while/body/eval_jaxpr/all_to_all | solution.py:89
  244.8 5.5 %all-to-all-done.1 = f32[4,1,64]{2,1,0:T(1,128)S(1)} async-done(((f32[4,1,64]{2,1,0:T(1,128)}), f32[4,1,64]{2,1,0:T(1,128)S(1)}, u32[]{:S(2)}, u32[]{:S(2)}) %all-to-all-start.1) | async-done | bytes 1056 | tf_op jit(solution)/shard_map/while/body/eval_jaxpr/all_to_all | solution.py:89
  250.2 20.5 %reduce-scatter.2.cloned.1.call-done = f32[4,64,768]{2,1,0:T(8,128)} async-done(((f32[4,64,3072]{2,1,0:T(8,128)}), f32[4,64,768]{2,1,0:T(8,128)}) %reduce-scatter.2.cloned.1.call-update) | async-done | bytes 786448 | tf_op jit(solution)/shard_map/while/body/eval_jaxpr/reduce_scatter | solution.py:86
  270.7 4.6 all-to-all-start.2
  276.9 6.1 %all-reduce.3 = (f32[80,2]{0,1:T(2,128)S(1)}, f32[80,4]{0,1:T(4,128)S(1)}) all-reduce(f32[80,2]{0,1:T(2,128)S(1)} %bitcast.182, f32[80,4]{0,1:T(4,128)S(1)} %fusion.126), channel_id=1, replica_groups=mesh['section'=2,'expert'=4,'tensor'=4] {'tensor'}, use_global_device_ids=true, to_apply=%region_11.11 | all-reduce | flops 480 | bytes 3840 | tf_op jit(solution)/shard_map/while/body/eval_jaxpr/psum | solution.py:101
  283.3 12.0 %all-to-all-done.2 = f32[4,64,768]{2,1,0:T(8,128)S(1)} async-done(((f32[4,64,768]{2,1,0:T(8,128)}), f32[4,64,768]{2,1,0:T(8,128)S(1)}, u32[]{:S(2)}, u32[]{:S(2)}) %all-to-all-start.2) | async-done | bytes 786464 | tf_op jit(solution)/shard_map/while/body/eval_jaxpr/all_to_all | solution.py:88
  296.0 5.9 %psum.63 = f32[80]{0:T(128)S(1)} all-reduce(f32[80]{0:T(128)S(1)} %get-tuple-element.643), channel_id=1, replica_groups=mesh['section'=2,'expert'=4,'tensor'=4] {'tensor'}, use_global_device_ids=true, to_apply=%region_13.13 | all-reduce | flops 80 | bytes 640 | tf_op jit(solution)/shard_map/while/body/eval_jaxpr/psum | solution.py:108
  302.1 1.3 collective-permute-start
  303.4 5.5 %collective-permute-done = bf16[80,768]{1,0:T(8,128)(2,1)S(1)} collective-permute-done((bf16[80,768]{1,0:T(8,128)(2,1)S(1)}, bf16[80,768]{1,0:T(8,128)(2,1)S(1)}, u32[]{:S(2)}, u32[]{:S(2)}) %collective-permute-start) | collective-permute-done | bytes 122912 | tf_op jit(solution)/shard_map/while/body/eval_jaxpr/ppermute | solution.py:13
  313.7 13.6 %all_to_all.47 = bf16[4,64,768]{2,1,0:T(8,128)(2,1)} all-to-all(bf16[4,64,768]{2,1,0:T(8,128)(2,1)S(1)} %bitcast.176), channel_id=1, replica_groups=mesh['section'=2,'expert'=4,'tensor'=4] {'expert'}, dimensions={0} | all-to-all | bytes 786432 | tf_op jit(solution)/shard_map/while/body/eval_jaxpr/all_to_all | solution.py:69
  327.4 17.3 %all-gather.6.cloned.1.call-done = bf16[16,64,768]{2,1,0:T(8,128)(2,1)} async-done(((bf16[4,64,768]{2,1,0:T(8,128)(2,1)}), bf16[16,64,768]{2,1,0:T(8,128)(2,1)}) %all-gather.6.cloned.1.call-update) | async-done | bytes 1572880 | tf_op jit(solution)/shard_map/while/body/eval_jaxpr/all_gather | solution.py:72
  344.7 2.6 copy.55
  348.5 9.7 %fusion.123 = (f32[4,64]{1,0:T(4,128)}, f32[4,64,2048]{2,1,0:T(8,128)S(1)}) fusion(bf16[1,2,4,64,2048]{4,3,2,1,0:T(8,128)(2,1)} %get-tuple-element.698, s32[]{:T(128)S(6)} %min.13, bf16[1,2,4,64,2048]{4,3,2,1,0:T(8,128)(2,1)} %get-tuple-element.699, bf16[4,64,3072]{2,1,0:T(8,128)(2,1)S(1)} %reshape.314, bf16[2048,3072]{1,0:T(8,128)(2,1)} %get-tuple-element.697), kind=kOutput, calls=%fused_computation.17.clone.1 | convolution fusion | flops 3225943808 | bytes 18351108 | tf_op jit(solution)/shard_map/while/body/eval_jaxpr/scw,fw->scf/dot_general | solution.py:39
  358.3 10.7 %fusion.129 = f32[4,64,3072]{2,1,0:T(8,128)} fusion(bf16[3072,2048]{1,0:T(8,128)(2,1)} %get-tuple-element.701, f32[4,64,2048]{2,1,0:T(8,128)S(1)} %get-tuple-element.640, bf16[1,2,4,64,2048]{4,3,2,1,0:T(8,128)(2,1)S(1)} %copy-done.6, s32[]{:T(128)S(6)} %min.13), kind=kOutput, calls=%fused_computation.2.clone.1 | convolution fusion | flops 3224895488 | bytes 18874372 | tf_op jit(solution)/shard_map/while/body/eval_jaxpr/scf,df->scd/dot_general | solution.py:84
  369.0 11.6 %fusion.130 = f32[4,64,3072]{2,1,0:T(8,128)} fusion(f32[4,64,3072]{2,1,0:T(8,128)} %fusion.129, bf16[3072,2048]{1,0:T(8,128)(2,1)} %get-tuple-element.700, f32[4,64,2048]{2,1,0:T(8,128)} %copy-done.8, bf16[1,2,4,64,2048]{4,3,2,1,0:T(8,128)(2,1)S(1)} %copy-done.7, s32[]{:T(128)S(6)} %min.13, bf16[1,2,4,64,2048]{4,3,2,1,0:T(8,128)(2,1)S(1)} %copy-done.5), kind=kOutput, calls=%fused_computation.8.clone.1 | convolution fusion | flops 3228303360 | bytes 23068676 | tf_op jit(solution)/shard_map/while/body/eval_jaxpr/scf,df->scd/dot_general | solution.py:83
  381.7 5.9 %psum.62 = f32[80]{0:T(128)S(1)} all-reduce(f32[80]{0:T(128)S(1)} %fusion.125), channel_id=1, replica_groups=mesh['section'=2,'expert'=4,'tensor'=4] {'tensor'}, use_global_device_ids=true, to_apply=%region_2.2 | all-reduce | flops 80 | bytes 640 | tf_op jit(solution)/shard_map/while/body/eval_jaxpr/psum | solution.py:43
  387.8 4.8 %all-to-all-start.1 = ((f32[4,1,64]{2,1,0:T(1,128)}), f32[4,1,64]{2,1,0:T(1,128)S(1)}, u32[]{:S(2)}, u32[]{:S(2)}) async-start(f32[4,1,64]{2,1,0:T(1,128)} %bitcast.168), calls=%async_computation.1 | async-start | bytes 4096 | tf_op jit(solution)/shard_map/while/body/eval_jaxpr/all_to_all | solution.py:89
  392.6 5.5 %all-to-all-done.1 = f32[4,1,64]{2,1,0:T(1,128)S(1)} async-done(((f32[4,1,64]{2,1,0:T(1,128)}), f32[4,1,64]{2,1,0:T(1,128)S(1)}, u32[]{:S(2)}, u32[]{:S(2)}) %all-to-all-start.1) | async-done | bytes 1056 | tf_op jit(solution)/shard_map/while/body/eval_jaxpr/all_to_all | solution.py:89
  398.1 20.5 %reduce-scatter.2.cloned.1.call-done = f32[4,64,768]{2,1,0:T(8,128)} async-done(((f32[4,64,3072]{2,1,0:T(8,128)}), f32[4,64,768]{2,1,0:T(8,128)}) %reduce-scatter.2.cloned.1.call-update) | async-done | bytes 786448 | tf_op jit(solution)/shard_map/while/body/eval_jaxpr/reduce_scatter | solution.py:86
  418.6 4.6 all-to-all-start.2
  424.7 6.1 %all-reduce.3 = (f32[80,2]{0,1:T(2,128)S(1)}, f32[80,4]{0,1:T(4,128)S(1)}) all-reduce(f32[80,2]{0,1:T(2,128)S(1)} %bitcast.182, f32[80,4]{0,1:T(4,128)S(1)} %fusion.126), channel_id=1, replica_groups=mesh['section'=2,'expert'=4,'tensor'=4] {'tensor'}, use_global_device_ids=true, to_apply=%region_11.11 | all-reduce | flops 480 | bytes 3840 | tf_op jit(solution)/shard_map/while/body/eval_jaxpr/psum | solution.py:101
  431.2 12.0 %all-to-all-done.2 = f32[4,64,768]{2,1,0:T(8,128)S(1)} async-done(((f32[4,64,768]{2,1,0:T(8,128)}), f32[4,64,768]{2,1,0:T(8,128)S(1)}, u32[]{:S(2)}, u32[]{:S(2)}) %all-to-all-start.2) | async-done | bytes 786464 | tf_op jit(solution)/shard_map/while/body/eval_jaxpr/all_to_all | solution.py:88
  443.8 5.9 %psum.63 = f32[80]{0:T(128)S(1)} all-reduce(f32[80]{0:T(128)S(1)} %get-tuple-element.643), channel_id=1, replica_groups=mesh['section'=2,'expert'=4,'tensor'=4] {'tensor'}, use_global_device_ids=true, to_apply=%region_13.13 | all-reduce | flops 80 | bytes 640 | tf_op jit(solution)/shard_map/while/body/eval_jaxpr/psum | solution.py:108
  451.3 5.5 %collective-permute-done = bf16[80,768]{1,0:T(8,128)(2,1)S(1)} collective-permute-done((bf16[80,768]{1,0:T(8,128)(2,1)S(1)}, bf16[80,768]{1,0:T(8,128)(2,1)S(1)}, u32[]{:S(2)}, u32[]{:S(2)}) %collective-permute-start) | collective-permute-done | bytes 122912 | tf_op jit(solution)/shard_map/while/body/eval_jaxpr/ppermute | solution.py:13
  (180 shorter events, 33.1 us)
Async XLA Ops:
  7.3 41.7 %all-gather.6.cloned.1.call-start = ((), (), s32[]{:S(2)}) async-start(), calls=%async_computation.4 | async-start | bytes 1966080 | tf_op jit(solution)/shard_map/while/body/eval_jaxpr/all_gather | solution.py:72
  30.1 92.8 %reduce-scatter.2.cloned.1.call-start = ((), (), s32[]{:S(2)}) async-start(), calls=%async_computation.5 | async-start | bytes 3932160 | tf_op jit(solution)/shard_map/while/body/eval_jaxpr/reduce_scatter | solution.py:86
  52.9 9.7 %copy-start.6 = (bf16[1,2,4,64,2048]{4,3,2,1,0:T(8,128)(2,1)S(1)}, bf16[1,2,4,64,2048]{4,3,2,1,0:T(8,128)(2,1)}, u32[]{:S(2)}) copy-start(bf16[1,2,4,64,2048]{4,3,2,1,0:T(8,128)(2,1)} %get-tuple-element.699) | copy-start | bytes 6291460 | tf_op jit(solution)/shard_map/while
  62.6 10.7 %copy-start.8 = (f32[4,64,2048]{2,1,0:T(8,128)}, f32[4,64,2048]{2,1,0:T(8,128)S(1)}, u32[]{:S(2)}) copy-start(f32[4,64,2048]{2,1,0:T(8,128)S(1)} %get-tuple-element.640) | copy-start | bytes 6291460 | tf_op jit(solution)/shard_map/while
  62.6 10.7 %copy-start.5 = (bf16[1,2,4,64,2048]{4,3,2,1,0:T(8,128)(2,1)S(1)}, bf16[1,2,4,64,2048]{4,3,2,1,0:T(8,128)(2,1)}, u32[]{:S(2)}) copy-start(bf16[1,2,4,64,2048]{4,3,2,1,0:T(8,128)(2,1)} %get-tuple-element.698) | copy-start | bytes 6291460 | tf_op jit(solution)/shard_map/while
  62.6 10.7 %copy-start.7 = (bf16[1,2,4,64,2048]{4,3,2,1,0:T(8,128)(2,1)S(1)}, bf16[1,2,4,64,2048]{4,3,2,1,0:T(8,128)(2,1)}, u32[]{:S(2)}) copy-start(bf16[1,2,4,64,2048]{4,3,2,1,0:T(8,128)(2,1)} %get-tuple-element.699) | copy-start | bytes 6291460 | tf_op jit(solution)/shard_map/while
  85.0 0.9 copy-start
  85.0 6.9 %copy-start.3 = (bf16[768,4]{0,1:T(4,128)(2,1)S(1)}, bf16[768,4]{0,1:T(4,128)(2,1)}, u32[]{:S(2)}) copy-start(bf16[768,4]{0,1:T(4,128)(2,1)} %get-tuple-element.696) | copy-start | bytes 18436 | tf_op jit(solution)/shard_map/while
  85.0 11.9 %copy-start.4 = (s32[1,2,80,2]{2,3,1,0:T(2,128)S(1)}, s32[1,2,80,2]{2,3,1,0:T(2,128)}, u32[]{:S(2)}) copy-start(s32[1,2,80,2]{2,3,1,0:T(2,128)} %get-tuple-element.694) | copy-start | bytes 3844 | tf_op jit(solution)/shard_map/while
  85.0 69.1 %copy-start.1 = (bf16[2,80,768]{2,1,0:T(8,128)(2,1)S(1)}, bf16[2,80,768]{2,1,0:T(8,128)(2,1)}, u32[]{:S(2)}) copy-start(bf16[2,80,768]{2,1,0:T(8,128)(2,1)} %get-tuple-element.692) | copy-start | bytes 737284 | tf_op jit(solution)/shard_map/while
  92.1 10.3 %all-to-all-start.1 = ((f32[4,1,64]{2,1,0:T(1,128)}), f32[4,1,64]{2,1,0:T(1,128)S(1)}, u32[]{:S(2)}, u32[]{:S(2)}) async-start(f32[4,1,64]{2,1,0:T(1,128)} %bitcast.168), calls=%async_computation.1 | async-start | bytes 4096 | tf_op jit(solution)/shard_map/while/body/eval_jaxpr/all_to_all | solution.py:89
  122.9 24.5 %all-to-all-start.2 = ((f32[4,64,768]{2,1,0:T(8,128)}), f32[4,64,768]{2,1,0:T(8,128)S(1)}, u32[]{:S(2)}, u32[]{:S(2)}) async-start(f32[4,64,768]{2,1,0:T(8,128)} %reduce-scatter.2.cloned.1.call-done), calls=%async_computation.3 | async-start | bytes 1572864 | tf_op jit(solution)/shard_map/while/body/eval_jaxpr/all_to_all | solution.py:88
  154.3 6.8 %collective-permute-start = (bf16[80,768]{1,0:T(8,128)(2,1)S(1)}, bf16[80,768]{1,0:T(8,128)(2,1)S(1)}, u32[]{:S(2)}, u32[]{:S(2)}) collective-permute-start(bf16[80,768]{1,0:T(8,128)(2,1)S(1)} %get-tuple-element.645), channel_id=1, source_target_pairs={{16,0},{17,1},{18,2},{19,3},{20,4},{21,5},{22,6},{23,7},{24,8},{25... | collective-permute-start | bytes 368648 | tf_op jit(solution)/shard_map/while/body/eval_jaxpr/ppermute | solution.py:13
  161.0 35.8 %all-gather.6.cloned.1.call-start = ((), (), s32[]{:S(2)}) async-start(), calls=%async_computation.4 | async-start | bytes 1966080 | tf_op jit(solution)/shard_map/while/body/eval_jaxpr/all_gather | solution.py:72
  179.5 91.2 %reduce-scatter.2.cloned.1.call-start = ((), (), s32[]{:S(2)}) async-start(), calls=%async_computation.5 | async-start | bytes 3932160 | tf_op jit(solution)/shard_map/while/body/eval_jaxpr/reduce_scatter | solution.py:86
  200.7 9.7 %copy-start.6 = (bf16[1,2,4,64,2048]{4,3,2,1,0:T(8,128)(2,1)S(1)}, bf16[1,2,4,64,2048]{4,3,2,1,0:T(8,128)(2,1)}, u32[]{:S(2)}) copy-start(bf16[1,2,4,64,2048]{4,3,2,1,0:T(8,128)(2,1)} %get-tuple-element.699) | copy-start | bytes 6291460 | tf_op jit(solution)/shard_map/while
  210.4 10.7 %copy-start.8 = (f32[4,64,2048]{2,1,0:T(8,128)}, f32[4,64,2048]{2,1,0:T(8,128)S(1)}, u32[]{:S(2)}) copy-start(f32[4,64,2048]{2,1,0:T(8,128)S(1)} %get-tuple-element.640) | copy-start | bytes 6291460 | tf_op jit(solution)/shard_map/while
  210.4 10.7 %copy-start.5 = (bf16[1,2,4,64,2048]{4,3,2,1,0:T(8,128)(2,1)S(1)}, bf16[1,2,4,64,2048]{4,3,2,1,0:T(8,128)(2,1)}, u32[]{:S(2)}) copy-start(bf16[1,2,4,64,2048]{4,3,2,1,0:T(8,128)(2,1)} %get-tuple-element.698) | copy-start | bytes 6291460 | tf_op jit(solution)/shard_map/while
  210.4 10.7 %copy-start.7 = (bf16[1,2,4,64,2048]{4,3,2,1,0:T(8,128)(2,1)S(1)}, bf16[1,2,4,64,2048]{4,3,2,1,0:T(8,128)(2,1)}, u32[]{:S(2)}) copy-start(bf16[1,2,4,64,2048]{4,3,2,1,0:T(8,128)(2,1)} %get-tuple-element.699) | copy-start | bytes 6291460 | tf_op jit(solution)/shard_map/while
  232.8 0.9 copy-start
  232.8 7.0 %copy-start.3 = (bf16[768,4]{0,1:T(4,128)(2,1)S(1)}, bf16[768,4]{0,1:T(4,128)(2,1)}, u32[]{:S(2)}) copy-start(bf16[768,4]{0,1:T(4,128)(2,1)} %get-tuple-element.696) | copy-start | bytes 18436 | tf_op jit(solution)/shard_map/while
  232.8 11.9 %copy-start.4 = (s32[1,2,80,2]{2,3,1,0:T(2,128)S(1)}, s32[1,2,80,2]{2,3,1,0:T(2,128)}, u32[]{:S(2)}) copy-start(s32[1,2,80,2]{2,3,1,0:T(2,128)} %get-tuple-element.694) | copy-start | bytes 3844 | tf_op jit(solution)/shard_map/while
  232.8 69.1 %copy-start.1 = (bf16[2,80,768]{2,1,0:T(8,128)(2,1)S(1)}, bf16[2,80,768]{2,1,0:T(8,128)(2,1)}, u32[]{:S(2)}) copy-start(bf16[2,80,768]{2,1,0:T(8,128)(2,1)} %get-tuple-element.692) | copy-start | bytes 737284 | tf_op jit(solution)/shard_map/while
  240.0 10.3 %all-to-all-start.1 = ((f32[4,1,64]{2,1,0:T(1,128)}), f32[4,1,64]{2,1,0:T(1,128)S(1)}, u32[]{:S(2)}, u32[]{:S(2)}) async-start(f32[4,1,64]{2,1,0:T(1,128)} %bitcast.168), calls=%async_computation.1 | async-start | bytes 4096 | tf_op jit(solution)/shard_map/while/body/eval_jaxpr/all_to_all | solution.py:89
  270.7 24.5 %all-to-all-start.2 = ((f32[4,64,768]{2,1,0:T(8,128)}), f32[4,64,768]{2,1,0:T(8,128)S(1)}, u32[]{:S(2)}, u32[]{:S(2)}) async-start(f32[4,64,768]{2,1,0:T(8,128)} %reduce-scatter.2.cloned.1.call-done), calls=%async_computation.3 | async-start | bytes 1572864 | tf_op jit(solution)/shard_map/while/body/eval_jaxpr/all_to_all | solution.py:88
  302.1 6.8 %collective-permute-start = (bf16[80,768]{1,0:T(8,128)(2,1)S(1)}, bf16[80,768]{1,0:T(8,128)(2,1)S(1)}, u32[]{:S(2)}, u32[]{:S(2)}) collective-permute-start(bf16[80,768]{1,0:T(8,128)(2,1)S(1)} %get-tuple-element.645), channel_id=1, source_target_pairs={{16,0},{17,1},{18,2},{19,3},{20,4},{21,5},{22,6},{23,7},{24,8},{25... | collective-permute-start | bytes 368648 | tf_op jit(solution)/shard_map/while/body/eval_jaxpr/ppermute | solution.py:13
  308.9 35.8 %all-gather.6.cloned.1.call-start = ((), (), s32[]{:S(2)}) async-start(), calls=%async_computation.4 | async-start | bytes 1966080 | tf_op jit(solution)/shard_map/while/body/eval_jaxpr/all_gather | solution.py:72
  327.4 91.2 %reduce-scatter.2.cloned.1.call-start = ((), (), s32[]{:S(2)}) async-start(), calls=%async_computation.5 | async-start | bytes 3932160 | tf_op jit(solution)/shard_map/while/body/eval_jaxpr/reduce_scatter | solution.py:86
  348.5 9.7 %copy-start.6 = (bf16[1,2,4,64,2048]{4,3,2,1,0:T(8,128)(2,1)S(1)}, bf16[1,2,4,64,2048]{4,3,2,1,0:T(8,128)(2,1)}, u32[]{:S(2)}) copy-start(bf16[1,2,4,64,2048]{4,3,2,1,0:T(8,128)(2,1)} %get-tuple-element.699) | copy-start | bytes 6291460 | tf_op jit(solution)/shard_map/while
  358.3 10.7 %copy-start.8 = (f32[4,64,2048]{2,1,0:T(8,128)}, f32[4,64,2048]{2,1,0:T(8,128)S(1)}, u32[]{:S(2)}) copy-start(f32[4,64,2048]{2,1,0:T(8,128)S(1)} %get-tuple-element.640) | copy-start | bytes 6291460 | tf_op jit(solution)/shard_map/while
  358.3 10.7 %copy-start.5 = (bf16[1,2,4,64,2048]{4,3,2,1,0:T(8,128)(2,1)S(1)}, bf16[1,2,4,64,2048]{4,3,2,1,0:T(8,128)(2,1)}, u32[]{:S(2)}) copy-start(bf16[1,2,4,64,2048]{4,3,2,1,0:T(8,128)(2,1)} %get-tuple-element.698) | copy-start | bytes 6291460 | tf_op jit(solution)/shard_map/while
  358.3 10.7 %copy-start.7 = (bf16[1,2,4,64,2048]{4,3,2,1,0:T(8,128)(2,1)S(1)}, bf16[1,2,4,64,2048]{4,3,2,1,0:T(8,128)(2,1)}, u32[]{:S(2)}) copy-start(bf16[1,2,4,64,2048]{4,3,2,1,0:T(8,128)(2,1)} %get-tuple-element.699) | copy-start | bytes 6291460 | tf_op jit(solution)/shard_map/while
  380.6 0.9 copy-start
  380.6 7.0 %copy-start.3 = (bf16[768,4]{0,1:T(4,128)(2,1)S(1)}, bf16[768,4]{0,1:T(4,128)(2,1)}, u32[]{:S(2)}) copy-start(bf16[768,4]{0,1:T(4,128)(2,1)} %get-tuple-element.696) | copy-start | bytes 18436 | tf_op jit(solution)/shard_map/while
  380.6 11.9 %copy-start.4 = (s32[1,2,80,2]{2,3,1,0:T(2,128)S(1)}, s32[1,2,80,2]{2,3,1,0:T(2,128)}, u32[]{:S(2)}) copy-start(s32[1,2,80,2]{2,3,1,0:T(2,128)} %get-tuple-element.694) | copy-start | bytes 3844 | tf_op jit(solution)/shard_map/while
  380.7 69.1 %copy-start.1 = (bf16[2,80,768]{2,1,0:T(8,128)(2,1)S(1)}, bf16[2,80,768]{2,1,0:T(8,128)(2,1)}, u32[]{:S(2)}) copy-start(bf16[2,80,768]{2,1,0:T(8,128)(2,1)} %get-tuple-element.692) | copy-start | bytes 737284 | tf_op jit(solution)/shard_map/while
  387.8 10.3 %all-to-all-start.1 = ((f32[4,1,64]{2,1,0:T(1,128)}), f32[4,1,64]{2,1,0:T(1,128)S(1)}, u32[]{:S(2)}, u32[]{:S(2)}) async-start(f32[4,1,64]{2,1,0:T(1,128)} %bitcast.168), calls=%async_computation.1 | async-start | bytes 4096 | tf_op jit(solution)/shard_map/while/body/eval_jaxpr/all_to_all | solution.py:89
  418.6 24.5 %all-to-all-start.2 = ((f32[4,64,768]{2,1,0:T(8,128)}), f32[4,64,768]{2,1,0:T(8,128)S(1)}, u32[]{:S(2)}, u32[]{:S(2)}) async-start(f32[4,64,768]{2,1,0:T(8,128)} %reduce-scatter.2.cloned.1.call-done), calls=%async_computation.3 | async-start | bytes 1572864 | tf_op jit(solution)/shard_map/while/body/eval_jaxpr/all_to_all | solution.py:88
  450.0 6.8 %collective-permute-start = (bf16[80,768]{1,0:T(8,128)(2,1)S(1)}, bf16[80,768]{1,0:T(8,128)(2,1)S(1)}, u32[]{:S(2)}, u32[]{:S(2)}) collective-permute-start(bf16[80,768]{1,0:T(8,128)(2,1)S(1)} %get-tuple-element.645), channel_id=1, source_target_pairs={{16,0},{17,1},{18,2},{19,3},{20,4},{21,5},{22,6},{23,7},{24,8},{25... | collective-permute-start | bytes 368648 | tf_op jit(solution)/shard_map/while/body/eval_jaxpr/ppermute | solution.py:13
  456.7 0.7 copy-start.2
Sparse Core Ops, SparseCore 0:
  30.3 18.7 all-gather.5
  85.1 37.7 reduce-scatter.1
  179.7 17.1 all-gather.5
  233.0 37.7 reduce-scatter.1
  327.5 17.1 all-gather.5
  380.8 37.7 reduce-scatter.1
